TPU v7x, 32 devices: a whole 2x2x4 slice. The times are simulated.
32 devices in a mesh: lat: 8 (over z, y), ch: 4 (over x, core).
Axes of the slice: x: 2, y: 2, z: 4, core: 2. Of those that a mesh axis runs over, the one named last changes fastest.
Arguments:
- state: float32 [1, 24, 180, 768], P(None, 'lat', None, 'ch'), may hold values from -30 to 30
- norm_gains: bfloat16 [2, 768], P(None, 'ch'), may hold values from 0.099609375 to 1.8984375
- channel_biases: bfloat16 [3, 768], P(None, 'ch'), may hold values from -2 to 2
- filter_in: float32 [2, 8, 96, 96], P(None, 'ch'), may hold values from -0.4375 to 0.4375
- filter_in_bias: float32 [2, 8, 96], P(None, 'ch'), may hold values from -2 to 2
- filter_out: float32 [2, 8, 96, 96], P(None, 'ch'), may hold values from -0.4375 to 0.4375
- filter_out_bias: float32 [2, 8, 96], P(None, 'ch'), may hold values from -2 to 2
- up_weight: bfloat16 [768, 3072], P(None, 'ch'), may hold values from -0.21875 to 0.21875
- up_bias: bfloat16 [3072], P('ch'), may hold values from -2 to 2
- down_weight: bfloat16 [3072, 768], P('ch'), may hold values from -0.109375 to 0.109375
Outputs:
- final_state: float32 [1, 24, 180, 768], P(None, 'lat', None, 'ch')
All inputs are finite; a program needn't handle non-finite values.
Results may differ from a plain program's by a relative error of at most 0.0012.
Values may be sent and summed in bfloat16 or wider, within the bound.
A program may use at most 128 MiB of HBM per device.

v0:
```python
import math

import jax
import jax.numpy as jnp
from jax import lax
from jax.sharding import PartitionSpec as P

D = 768
M = 64
STEPS = 4


EPS = 1e-05
SHRINK = 0.01
HIGH = lax.Precision.HIGHEST


def longitude_tables(width, modes):
    column = jnp.arange(width, dtype=jnp.int32)[:, None]
    order = jnp.arange(modes, dtype=jnp.int32)[None, :]
    angle = 2.0 * math.pi / width * (column * order % width).astype(jnp.float32)
    doubled = jnp.where(order == 0, 1.0, 2.0).astype(jnp.float32)
    return (jnp.cos(angle), jnp.sin(angle), jnp.cos(angle) * doubled, jnp.sin(angle) * doubled)


def latitude_tables(height):
    column = jnp.arange(height, dtype=jnp.int32)[:, None]
    order = jnp.arange(height, dtype=jnp.int32)[None, :]
    angle = 2.0 * math.pi / height * (column * order % height).astype(jnp.float32)
    return (jnp.cos(angle), jnp.sin(angle))


def layer_norm(values, gain, shift):
    mean = jnp.sum(values, -1, keepdims=True) / values.shape[-1]
    spread = jnp.sum(values * values, -1, keepdims=True) / values.shape[-1] - mean * mean
    return (values - mean) * lax.rsqrt(spread + EPS) * gain + shift


def soft_shrink(values):
    return jnp.where(
        values > SHRINK, values - SHRINK, jnp.where(values < -SHRINK, values + SHRINK, 0.0)
    )


def block_apply(left, matrix):
    return jnp.einsum("bkmnj,nji->bkmni", left, matrix, precision=HIGH)


def spectral_mlp(real_part, imag_part, filter_in, filter_in_bias, filter_out, filter_out_bias):
    shape = real_part.shape
    blocks = filter_in.shape[1]
    size = filter_in.shape[2]
    real_blocks = real_part.reshape(shape[:-1] + (blocks, size))
    imag_blocks = imag_part.reshape(shape[:-1] + (blocks, size))
    first_real = jax.nn.relu(
        block_apply(real_blocks, filter_in[0])
        - block_apply(imag_blocks, filter_in[1])
        + filter_in_bias[0]
    )
    first_imag = jax.nn.relu(
        block_apply(imag_blocks, filter_in[0])
        + block_apply(real_blocks, filter_in[1])
        + filter_in_bias[1]
    )
    second_real = (
        block_apply(first_real, filter_out[0])
        - block_apply(first_imag, filter_out[1])
        + filter_out_bias[0]
    )
    second_imag = (
        block_apply(first_imag, filter_out[0])
        + block_apply(first_real, filter_out[1])
        + filter_out_bias[1]
    )
    return (soft_shrink(second_real).reshape(shape), soft_shrink(second_imag).reshape(shape))


def local(
    state,
    norm_gains,
    channel_biases,
    filter_in,
    filter_in_bias,
    filter_out,
    filter_out_bias,
    up_weight,
    up_bias,
    down_weight,
):
    width = state.shape[2]
    height = state.shape[1] * lax.axis_size("lat")
    scale = 1.0 / math.sqrt(height * width)
    lon_cos, lon_sin, back_cos, back_sin = longitude_tables(width, M)
    lat_cos, lat_sin = latitude_tables(height)
    gains = norm_gains.astype(jnp.float32)
    shifts = channel_biases.astype(jnp.float32)
    full_up, full_gains, full_biases = (
        lax.all_gather(up_weight, "ch", axis=1, tiled=True),
        lax.all_gather(norm_gains, "ch", axis=1, tiled=True),
        lax.all_gather(channel_biases, "ch", axis=1, tiled=True),
    )
    full_down, full_up_bias = (
        lax.all_gather(down_weight, "ch", axis=0, tiled=True),
        lax.all_gather(up_bias, "ch", axis=0, tiled=True),
    )
    wide_gains = full_gains.astype(jnp.float32)
    wide_biases = full_biases.astype(jnp.float32)
    wide_up_bias = full_up_bias.astype(jnp.float32)
    values = state
    for step_index in range(STEPS):
        total, squares = lax.psum(
            (jnp.sum(values, -1, keepdims=True), jnp.sum(values * values, -1, keepdims=True)), "ch"
        )
        mean = total / D
        mean, spread = (mean, squares / D - mean * mean)
        normed = (values - mean) * lax.rsqrt(spread + EPS) * gains[0] + shifts[0]
        real_lon = jnp.einsum("bhwd,wm->bhmd", normed, lon_cos, precision=HIGH)
        imag_lon = -jnp.einsum("bhwd,wm->bhmd", normed, lon_sin, precision=HIGH)
        stacked = lax.all_to_all(
            jnp.stack((real_lon, imag_lon)), "lat", split_axis=3, concat_axis=2, tiled=True
        )
        spectral_real_lon = stacked[0]
        spectral_imag_lon = stacked[1]
        real_spec = (
            jnp.einsum("kh,bhmd->bkmd", lat_cos, spectral_real_lon, precision=HIGH)
            + jnp.einsum("kh,bhmd->bkmd", lat_sin, spectral_imag_lon, precision=HIGH)
        ) * scale
        imag_spec = (
            jnp.einsum("kh,bhmd->bkmd", lat_cos, spectral_imag_lon, precision=HIGH)
            - jnp.einsum("kh,bhmd->bkmd", lat_sin, spectral_real_lon, precision=HIGH)
        ) * scale
        out_real, out_imag = spectral_mlp(
            real_spec, imag_spec, filter_in, filter_in_bias, filter_out, filter_out_bias
        )
        real_rows = jnp.einsum("kh,bkmd->bhmd", lat_cos, out_real, precision=HIGH) - jnp.einsum(
            "kh,bkmd->bhmd", lat_sin, out_imag, precision=HIGH
        )
        imag_rows = jnp.einsum("kh,bkmd->bhmd", lat_cos, out_imag, precision=HIGH) + jnp.einsum(
            "kh,bkmd->bhmd", lat_sin, out_real, precision=HIGH
        )
        rows = lax.all_to_all(
            jnp.stack((real_rows, imag_rows)), "lat", split_axis=2, concat_axis=3, tiled=True
        )
        back = jnp.einsum("bhmd,wm->bhwd", rows[0], back_cos, precision=HIGH) - jnp.einsum(
            "bhmd,wm->bhwd", rows[1], back_sin, precision=HIGH
        )
        values = values + back * scale + normed
        owned = lax.all_to_all(values, "ch", split_axis=2, concat_axis=3, tiled=True)
        normed_two = layer_norm(owned, wide_gains[1], wide_biases[1]).astype(jnp.bfloat16)
        flat = normed_two.reshape(-1, normed_two.shape[-1])
        pre = jnp.dot(flat, full_up, preferred_element_type=jnp.float32) + wide_up_bias
        hidden = jax.nn.gelu(pre, approximate=False).astype(jnp.bfloat16)
        mixed = jnp.dot(hidden, full_down, preferred_element_type=jnp.float32) + wide_biases[2]
        values = values + lax.all_to_all(
            mixed.reshape(owned.shape), "ch", split_axis=3, concat_axis=2, tiled=True
        )
    return values


def solution(mesh):
    placed = (
        P(None, "lat", None, "ch"),
        P(None, "ch"),
        P(None, "ch"),
        P(None, "ch", None, None),
        P(None, "ch", None),
        P(None, "ch", None, None),
        P(None, "ch", None),
        P(None, "ch"),
        P("ch"),
        P("ch", None),
    )
    return jax.shard_map(
        local, mesh=mesh, in_specs=placed, out_specs=P(None, "lat", None, "ch"), check_vma=False
    )
```

profile of v0, /device:TPU:0, one launch (start us, length us, event | category | flops | bytes accessed | tf_op | source)
XLA Modules:
  0.0 448.4 jit_solution(3237822838711945097)
XLA Ops:
  10.7 8.5 %all-reduce.3 = (f32[1,3,180,1]{2,1,3,0:T(4,128)S(1)}, f32[1,3,180,1]{2,1,3,0:T(4,128)S(1)}) all-reduce(f32[1,3,180,1]{2,1,3,0:T(4,128)S(1)} %bitcast.885, f32[1,3,180,1]{2,1,3,0:T(4,128)S(1)} %bitcast.884), channel_id=1, replica_groups=mesh['lat'=8,'ch'=4] {'ch'}, use_global_device_ids=true, to_apply=%region_3.4 | all-reduce | flops 1080 | bytes 8640 | tf_op jit(solution)/shard_map/psum | solution.py:111
  22.0 5.8 %all-to-all-start = ((f32[2,1,3,64,192]{4,0,2,1,3:T(2,128)}), f32[2,1,3,64,192]{4,0,2,1,3:T(2,128)S(1)}, u32[]{:S(2)}, u32[]{:S(2)}) async-start(f32[2,1,3,64,192]{4,0,2,1,3:T(2,128)} %copy.567), calls=%async_computation | async-start | bytes 786432 | tf_op jit(solution)/shard_map/all_to_all | solution.py:119
  27.9 10.4 %all-to-all-done = f32[2,1,3,64,192]{4,0,2,1,3:T(2,128)S(1)} async-done(((f32[2,1,3,64,192]{4,0,2,1,3:T(2,128)}), f32[2,1,3,64,192]{4,0,2,1,3:T(2,128)S(1)}, u32[]{:S(2)}, u32[]{:S(2)}) %all-to-all-start) | async-done | bytes 294944 | tf_op jit(solution)/shard_map/all_to_all | solution.py:119
  50.0 5.1 %all-gather = bf16[4,192,2]{1,2,0:T(2,128)(2,1)S(1)} all-gather(bf16[1,192,2]{1,2,0:T(2,128)(2,1)S(1)} %bitcast.892), channel_id=1, replica_groups=mesh['lat'=8,'ch'=4] {'ch'}, dimensions={0}, use_global_device_ids=true | all-gather | bytes 3840 | tf_op jit(solution)/shard_map/all_gather | solution.py:99
  55.2 5.4 %all-gather.1 = bf16[4,192,3]{1,2,0:T(4,128)(2,1)S(1)} all-gather(bf16[1,192,3]{1,2,0:T(4,128)(2,1)S(1)} %bitcast.891), channel_id=1, replica_groups=mesh['lat'=8,'ch'=4] {'ch'}, dimensions={0}, use_global_device_ids=true | all-gather | bytes 5760 | tf_op jit(solution)/shard_map/all_gather | solution.py:100
  67.9 16.5 %all-gather.2 = bf16[4,1,768]{2,1,0:T(2,128)(2,1)S(1)} all-gather(bf16[1,1,768]{2,1,0:T(2,128)(2,1)S(1)} %reshape.758), channel_id=1, replica_groups=mesh['lat'=8,'ch'=4] {'ch'}, dimensions={0}, use_global_device_ids=true | all-gather | bytes 7680 | tf_op jit(solution)/shard_map/all_gather | solution.py:104
  86.8 7.3 %all-gather.8.cloned.1.call-done = bf16[3072,768]{1,0:T(8,128)(2,1)} async-done(((bf16[768,768]{1,0:T(8,128)(2,1)}), bf16[3072,768]{1,0:T(8,128)(2,1)}) %all-gather.8.cloned.1.call-update) | async-done | bytes 4718608 | tf_op jit(solution)/shard_map/all_gather | solution.py:103
  94.1 8.7 %convolution_add_fusion.7 = f32[135,768]{1,0:T(8,128)S(1)} fusion(bf16[3072,768]{1,0:T(8,128)(2,1)} %all-gather.8.cloned.1.call-done, bf16[768,3072]{1,0:T(8,128)(2,1)} %all-gather.6.cloned.1.call-done, f32[3072]{0:T(1024)S(1)} %bitcast.886, f32[135,768]{1,0:T(8,128)S(1)} %all_to_all.201, f32[768]{0:T(1024)S(1)} %get-tuple-element.22, ...), kind=kOutput, calls=%fused_computation.103 | convolution fusion | flops 1302013440 | bytes 10289208 | tf_op jit(solution)/shard_map/dot_general | solution.py:153
  106.0 5.2 %reduce.38 = f32[768,3,45]{2,1,0:T(4,128)S(1)} reduce(f32[768,3,1,45]{3,2,1,0:T(1,128)} %bitcast.817, f32[]{:T(128)} %broadcast.994), dimensions={2}, to_apply=%bitcast.749.reduce_sub_computation | reduce | bytes 829444
  112.8 10.4 %all_to_all.264 = f32[4,1,25920]{2,1,0:T(1,128)S(1)} all-to-all(f32[4,1,25920]{2,1,0:T(1,128)S(1)} %reshape.803), channel_id=1, replica_groups=mesh['lat'=8,'ch'=4] {'ch'}, dimensions={0} | all-to-all | bytes 829440 | tf_op jit(solution)/shard_map/all_to_all | solution.py:154
  128.4 4.9 %bitcast_reduce_fusion.3 = f32[3,45,768]{1,0,2:T(4,128)S(1)} fusion(f32[768,3,1,45]{3,2,1,0:T(1,128)} %reshape.804), kind=kLoop, calls=%fused_computation.1077 | loop fusion | bytes 829440 | tf_op jit(solution)/shard_map/all_to_all | solution.py:154
  135.1 5.9 %all-reduce.2 = (f32[1,3,180,1]{2,1,3,0:T(4,128)S(1)}, f32[1,3,180,1]{2,1,3,0:T(4,128)S(1)}) all-reduce(f32[1,3,180,1]{2,1,3,0:T(4,128)S(1)} %bitcast.879, f32[1,3,180,1]{2,1,3,0:T(4,128)S(1)} %bitcast.878), channel_id=1, replica_groups=mesh['lat'=8,'ch'=4] {'ch'}, use_global_device_ids=true, to_apply=%region_9.10 | all-reduce | flops 1080 | bytes 8640 | tf_op jit(solution)/shard_map/psum | solution.py:111
  143.1 17.5 %all_to_all.265 = f32[2,1,3,64,192]{4,0,2,1,3:T(2,128)S(1)} all-to-all(f32[2,1,3,64,192]{4,0,2,1,3:T(2,128)S(1)} %copy.603), channel_id=1, replica_groups=mesh['lat'=8,'ch'=4] {'lat'}, dimensions={3} | all-to-all | bytes 589824 | tf_op jit(solution)/shard_map/all_to_all | solution.py:119
  167.8 14.9 %all_to_all.266 = f32[2,1,24,8,192]{4,3,1,0,2:T(8,128)S(1)} all-to-all(f32[2,1,24,8,192]{4,3,1,0,2:T(8,128)S(1)} %copy.625), channel_id=1, replica_groups=mesh['lat'=8,'ch'=4] {'lat'}, dimensions={2} | all-to-all | bytes 589824 | tf_op jit(solution)/shard_map/all_to_all | solution.py:141
  185.3 11.7 %all_to_all.267 = f32[1,3,180,192]{3,0,1,2:T(1,128)S(1)} all-to-all(f32[1,3,180,192]{3,0,1,2:T(1,128)S(1)} %copy.629), channel_id=1, replica_groups=mesh['lat'=8,'ch'=4] {'ch'}, dimensions={2} | all-to-all | bytes 829440 | tf_op jit(solution)/shard_map/all_to_all | solution.py:148
  199.2 8.7 %convolution_add_fusion.6 = f32[135,768]{1,0:T(8,128)S(1)} fusion(bf16[3072,768]{1,0:T(8,128)(2,1)} %all-gather.8.cloned.1.call-done, bf16[768,3072]{1,0:T(8,128)(2,1)} %all-gather.6.cloned.1.call-done, f32[3072]{0:T(1024)S(1)} %bitcast.887, f32[135,768]{1,0:T(8,128)S(1)} %all_to_all.215, f32[135]{0:T(256)S(1)} %add_rsqrt_fusion.2, f32[135]{0:T(256)S(1)} %div.73, ...), kind=kOutput, calls=%fused_computation.102 | convolution fusion | flops 1302013440 | bytes 10289208 | tf_op jit(solution)/shard_map/dot_general | solution.py:153
  210.6 5.2 %reduce.40 = f32[768,3,45]{2,1,0:T(4,128)S(1)} reduce(f32[768,3,1,45]{3,2,1,0:T(1,128)} %bitcast.818, f32[]{:T(128)} %broadcast.994), dimensions={2}, to_apply=%bitcast.751.reduce_sub_computation | reduce | bytes 829444
  217.5 10.4 %all_to_all.268 = f32[4,1,25920]{2,1,0:T(1,128)S(1)} all-to-all(f32[4,1,25920]{2,1,0:T(1,128)S(1)} %reshape.805), channel_id=1, replica_groups=mesh['lat'=8,'ch'=4] {'ch'}, dimensions={0} | all-to-all | bytes 829440 | tf_op jit(solution)/shard_map/all_to_all | solution.py:154
  233.0 4.9 %bitcast_reduce_fusion.2 = f32[3,45,768]{1,0,2:T(4,128)S(1)} fusion(f32[768,3,1,45]{3,2,1,0:T(1,128)} %reshape.806), kind=kLoop, calls=%fused_computation.1076 | loop fusion | bytes 829440 | tf_op jit(solution)/shard_map/all_to_all | solution.py:154
  239.8 5.9 %all-reduce.1 = (f32[1,3,180,1]{2,1,3,0:T(4,128)S(1)}, f32[1,3,180,1]{2,1,3,0:T(4,128)S(1)}) all-reduce(f32[1,3,180,1]{2,1,3,0:T(4,128)S(1)} %bitcast.881, f32[1,3,180,1]{2,1,3,0:T(4,128)S(1)} %bitcast.880), channel_id=1, replica_groups=mesh['lat'=8,'ch'=4] {'ch'}, use_global_device_ids=true, to_apply=%region_15.16 | all-reduce | flops 1080 | bytes 8640 | tf_op jit(solution)/shard_map/psum | solution.py:111
  247.7 15.2 %all_to_all.269 = f32[2,1,3,64,192]{4,0,2,1,3:T(2,128)S(1)} all-to-all(f32[2,1,3,64,192]{4,0,2,1,3:T(2,128)S(1)} %copy.636), channel_id=1, replica_groups=mesh['lat'=8,'ch'=4] {'lat'}, dimensions={3} | all-to-all | bytes 589824 | tf_op jit(solution)/shard_map/all_to_all | solution.py:119
  270.1 14.9 %all_to_all.270 = f32[2,1,24,8,192]{4,3,1,0,2:T(8,128)S(1)} all-to-all(f32[2,1,24,8,192]{4,3,1,0,2:T(8,128)S(1)} %copy.658), channel_id=1, replica_groups=mesh['lat'=8,'ch'=4] {'lat'}, dimensions={2} | all-to-all | bytes 589824 | tf_op jit(solution)/shard_map/all_to_all | solution.py:141
  287.6 11.7 %all_to_all.271 = f32[1,3,180,192]{3,0,1,2:T(1,128)S(1)} all-to-all(f32[1,3,180,192]{3,0,1,2:T(1,128)S(1)} %copy.662), channel_id=1, replica_groups=mesh['lat'=8,'ch'=4] {'ch'}, dimensions={2} | all-to-all | bytes 829440 | tf_op jit(solution)/shard_map/all_to_all | solution.py:148
  301.6 8.7 %convolution_add_fusion.5 = f32[135,768]{1,0:T(8,128)S(1)} fusion(bf16[3072,768]{1,0:T(8,128)(2,1)} %all-gather.8.cloned.1.call-done, bf16[768,3072]{1,0:T(8,128)(2,1)} %all-gather.6.cloned.1.call-done, f32[3072]{0:T(1024)S(1)} %bitcast.888, f32[135,768]{1,0:T(8,128)S(1)} %all_to_all.229, f32[135]{0:T(256)S(1)} %add_rsqrt_fusion.1, f32[135]{0:T(256)S(1)} %div.79, ...), kind=kOutput, calls=%fused_computation.101 | convolution fusion | flops 1302013440 | bytes 10289208 | tf_op jit(solution)/shard_map/dot_general | solution.py:153
  313.0 5.2 %reduce.42 = f32[768,3,45]{2,1,0:T(4,128)S(1)} reduce(f32[768,3,1,45]{3,2,1,0:T(1,128)} %bitcast.819, f32[]{:T(128)} %broadcast.994), dimensions={2}, to_apply=%bitcast.753.reduce_sub_computation | reduce | bytes 829444
  319.8 10.4 %all_to_all.272 = f32[4,1,25920]{2,1,0:T(1,128)S(1)} all-to-all(f32[4,1,25920]{2,1,0:T(1,128)S(1)} %reshape.807), channel_id=1, replica_groups=mesh['lat'=8,'ch'=4] {'ch'}, dimensions={0} | all-to-all | bytes 829440 | tf_op jit(solution)/shard_map/all_to_all | solution.py:154
  342.1 5.9 %all-reduce = (f32[1,3,180,1]{2,1,3,0:T(4,128)S(1)}, f32[1,3,180,1]{2,1,3,0:T(4,128)S(1)}) all-reduce(f32[1,3,180,1]{2,1,3,0:T(4,128)S(1)} %bitcast.883, f32[1,3,180,1]{2,1,3,0:T(4,128)S(1)} %bitcast.882), channel_id=1, replica_groups=mesh['lat'=8,'ch'=4] {'ch'}, use_global_device_ids=true, to_apply=%region_21.22 | all-reduce | flops 1080 | bytes 8640 | tf_op jit(solution)/shard_map/psum | solution.py:111
  350.0 15.2 %all_to_all.273 = f32[2,1,3,64,192]{4,0,2,1,3:T(2,128)S(1)} all-to-all(f32[2,1,3,64,192]{4,0,2,1,3:T(2,128)S(1)} %copy.669), channel_id=1, replica_groups=mesh['lat'=8,'ch'=4] {'lat'}, dimensions={3} | all-to-all | bytes 589824 | tf_op jit(solution)/shard_map/all_to_all | solution.py:119
  372.5 14.9 %all_to_all.274 = f32[2,1,24,8,192]{4,3,1,0,2:T(8,128)S(1)} all-to-all(f32[2,1,24,8,192]{4,3,1,0,2:T(8,128)S(1)} %copy.691), channel_id=1, replica_groups=mesh['lat'=8,'ch'=4] {'lat'}, dimensions={2} | all-to-all | bytes 589824 | tf_op jit(solution)/shard_map/all_to_all | solution.py:141
  390.0 11.7 %all_to_all.275 = f32[1,3,180,192]{3,0,1,2:T(1,128)S(1)} all-to-all(f32[1,3,180,192]{3,0,1,2:T(1,128)S(1)} %copy.695), channel_id=1, replica_groups=mesh['lat'=8,'ch'=4] {'ch'}, dimensions={2} | all-to-all | bytes 829440 | tf_op jit(solution)/shard_map/all_to_all | solution.py:148
  404.0 8.7 %convolution_add_fusion.4 = f32[135,768]{1,0:T(8,128)S(1)} fusion(bf16[3072,768]{1,0:T(8,128)(2,1)} %all-gather.8.cloned.1.call-done, bf16[768,3072]{1,0:T(8,128)(2,1)} %all-gather.6.cloned.1.call-done, f32[3072]{0:T(1024)S(1)} %bitcast.889, f32[135,768]{1,0:T(8,128)S(1)} %all_to_all.243, f32[135]{0:T(256)S(1)} %add_rsqrt_fusion, f32[135]{0:T(256)S(1)} %div.85, ...), kind=kOutput, calls=%fused_computation.100 | convolution fusion | flops 1302013440 | bytes 10289208 | tf_op jit(solution)/shard_map/dot_general | solution.py:153
  420.3 10.0 %all_to_all.276 = f32[4,1,25920]{2,1,0:T(1,128)S(1)} all-to-all(f32[4,1,25920]{2,1,0:T(1,128)S(1)} %reshape.809), channel_id=1, replica_groups=mesh['lat'=8,'ch'=4] {'ch'}, dimensions={0} | all-to-all | bytes 829440 | tf_op jit(solution)/shard_map/all_to_all | solution.py:154
  (263 shorter events, 127.3 us)
Async XLA Ops:
  6.5 1.5 copy-start.3
  6.5 1.5 copy-start.2
  6.5 12.7 %copy-start.4 = (bf16[2,192]{1,0:T(2,128)(2,1)S(1)}, bf16[2,192]{1,0:T(2,128)(2,1)}, u32[]{:S(2)}) copy-start(bf16[2,192]{1,0:T(2,128)(2,1)} %param.11) | copy-start | bytes 2308
  6.5 80.3 %all-gather.6.cloned.1.call-start = ((), (), s32[]{:S(2)}) async-start(), calls=%async_computation.16 | async-start | bytes 5898240 | tf_op jit(solution)/shard_map/all_gather | solution.py:98
  7.3 86.8 %all-gather.8.cloned.1.call-start = ((), (), s32[]{:S(2)}) async-start(), calls=%async_computation.17 | async-start | bytes 5898240 | tf_op jit(solution)/shard_map/all_gather | solution.py:103
  20.1 7.8 %copy-start.5 = (f32[2,2,96]{2,1,0:T(2,128)S(1)}, f32[2,2,96]{2,1,0:T(2,128)}, u32[]{:S(2)}) copy-start(f32[2,2,96]{2,1,0:T(2,128)} %param.14) | copy-start | bytes 4612
  20.1 7.8 %copy-start.6 = (f32[2,2,96]{2,1,0:T(2,128)S(1)}, f32[2,2,96]{2,1,0:T(2,128)}, u32[]{:S(2)}) copy-start(f32[2,2,96]{2,1,0:T(2,128)} %param.16) | copy-start | bytes 4612
  22.0 16.2 %all-to-all-start = ((f32[2,1,3,64,192]{4,0,2,1,3:T(2,128)}), f32[2,1,3,64,192]{4,0,2,1,3:T(2,128)S(1)}, u32[]{:S(2)}, u32[]{:S(2)}) async-start(f32[2,1,3,64,192]{4,0,2,1,3:T(2,128)} %copy.567), calls=%async_computation | async-start | bytes 786432 | tf_op jit(solution)/shard_map/all_to_all | solution.py:119
  38.4 2.2 copy-start
  39.9 1.9 copy-start.1
  44.7 5.4 %copy-start.7 = (bf16[768]{0:T(1024)(128)(2,1)S(1)}, bf16[768]{0:T(1024)(128)(2,1)}, u32[]{:S(2)}) copy-start(bf16[768]{0:T(1024)(128)(2,1)} %param.18) | copy-start | bytes 4612
  46.3 14.6 %all-to-all-start.1 = ((f32[2,1,24,8,192]{4,3,1,0,2:T(8,128)}), f32[2,1,24,8,192]{4,3,1,0,2:T(8,128)S(1)}, u32[]{:S(2)}, u32[]{:S(2)}) async-start(f32[2,1,24,8,192]{4,3,1,0,2:T(8,128)} %copy.589), calls=%async_computation.1 | async-start | bytes 786432 | tf_op jit(solution)/shard_map/all_to_all | solution.py:141
  64.3 20.1 %all-to-all-start.2 = ((f32[1,3,180,192]{3,0,1,2:T(1,128)}), f32[1,3,180,192]{3,0,1,2:T(1,128)S(1)}, u32[]{:S(2)}, u32[]{:S(2)}) async-start(f32[1,3,180,192]{3,0,1,2:T(1,128)} %copy.594), calls=%async_computation.2 | async-start | bytes 1105920 | tf_op jit(solution)/shard_map/all_to_all | solution.py:148
Sparse Core Ops, SparseCore 0:
  8.9 40.1 all-gather.5
  50.6 43.4 all-gather.7
where the time goes:
time: 457 us; the launch traced here: 448 us
  blocking collectives  222 us (49%)
  matrix products  72.4 us (16%)
  local copies, waits for them, and re-layouts  69.2 us (15%)
  other arithmetic  36.9 us (8%)
  waiting for transfers between devices  19.4 us (4%)
  between operations  15.4 us (3%)
  starting transfers between devices  13 us (3%)
    all_to_all x3, blocking collectives, local(): lax.all_to_all(jnp.stack((real_lon, imag_lon)), 'lat', split_axis=3, conc...  47.8 us
    all_to_all x3, blocking collectives, local(): lax.all_to_all(jnp.stack((real_rows, imag_rows)), 'lat', split_axis=2, co...  44.7 us
    all_to_all x4, blocking collectives, local(): lax.all_to_all(mixed.reshape(owned.shape), 'ch', split_axis=3, concat_axi...  41.2 us
    all_to_all x3, blocking collectives, local(): lax.all_to_all(values, 'ch', split_axis=2, concat_axis=3, tiled=True)  35.1 us
    dot_general x4, matrix products, local(): jnp.dot(hidden, full_down, preferred_element_type=jnp.float32)  34.7 us
    psum x4, blocking collectives, local(): lax.psum((jnp.sum(values, -1, keepdims=True), jnp.sum(values * values, -1...  26.2 us
    all_to_all x12, local copies, waits for them, and re-layouts, local(): lax.all_to_all(mixed.reshape(owned.shape), 'ch', split_axis=3, concat_axi...  24.4 us
    unnamed x4, other arithmetic  20.4 us
  transfers between devices with their start and end apart: 5, of which 3 were waited for; matrix products, arithmetic and copies ran while one was open for 4% of the time, Pallas kernels for 0%

commit v1 on v0

--- a/solution.py
+++ b/solution.py
@@ -1,8 +1,12 @@
+import functools
 import math
 
 import jax
 import jax.numpy as jnp
 from jax import lax
+import numpy as np
+from jax.experimental import pallas as pl
+from jax.experimental.pallas import tpu as pltpu
 from jax.sharding import PartitionSpec as P
 
 D = 768
@@ -157,6 +161,389 @@
     return values
 
 
+PIECES = 2
+F32 = jnp.float32
+BF16 = jnp.bfloat16
+MESH = pl.DeviceIdType.MESH
+
+
+def split_table(table):
+    high = np.asarray(table, np.float32).astype(jnp.bfloat16)
+    low = (table - high.astype(np.float64)).astype(np.float32).astype(jnp.bfloat16)
+    return np.stack((high, low))
+
+
+def fourier_tables(width, padded, height, modes, owners):
+    scale = 1.0 / math.sqrt(height * width)
+    share = modes // owners
+    order = np.arange(modes).reshape(owners, share)
+    angle = 2.0 * np.pi / width * (order[:, :, None] * np.arange(width) % width)
+    forward = np.zeros((owners, 2, share, padded))
+    forward[:, 0, :, :width] = np.cos(angle)
+    forward[:, 1, :, :width] = -np.sin(angle)
+    doubled = np.where(order == 0, 1.0, 2.0)[:, None, :, None] * scale
+    backward = (forward * doubled).reshape(2 * modes, padded).T
+    forward = forward.reshape(2 * modes, padded)
+    rows = np.arange(height)
+    turn = 2.0 * np.pi / height * (rows[:, None] * rows[None, :] % height)
+    cos, sin, eye = np.cos(turn), np.sin(turn), np.eye(share)
+    mix = np.array([[cos, sin], [-sin, cos]])
+    size = 2 * height * share
+    lat = np.einsum("abkh,mn->akmhbn", mix, eye).reshape(size, size) * scale
+    unmix = np.array([[cos, -sin], [sin, cos]])
+    back = np.einsum("bahk,mn->hbmakn", unmix, eye).reshape(size, size)
+    return tuple(split_table(t) for t in (forward, lat, back, backward))
+
+
+def dot(left, right):
+    return jnp.dot(left, right, preferred_element_type=F32)
+
+
+def halves(values):
+    high = values.astype(BF16)
+    return high, (values - high.astype(F32)).astype(BF16)
+
+
+def gelu(values):
+    return 0.5 * values * (1.0 + lax.erf(values * (1.0 / math.sqrt(2.0))))
+
+
+def rollout(
+    lats,
+    chans,
+    state,
+    gains,
+    shifts,
+    fin,
+    fin_bias,
+    fout,
+    fout_bias,
+    up,
+    up_bias,
+    down,
+    t_lon,
+    t_lat,
+    t_rows,
+    t_back,
+    out,
+    x,
+    stat_send,
+    stat_recv,
+    lon_send,
+    lon_recv,
+    row_send,
+    row_recv,
+    tok_send,
+    tok_recv,
+    mix_send,
+    mix_recv,
+    bias_send,
+    bias_recv,
+    up_recv,
+    down_recv,
+    partial,
+    hidden,
+    mixing,
+    send_sem,
+    recv_sem,
+):
+    lat, ch = lax.axis_index("lat"), lax.axis_index("ch")
+    core = lax.rem(ch, 2)
+    partner = ch + 1 - 2 * core
+    rows, width, own = state.shape
+    padded = x.shape[0] // rows
+    half = x.shape[0] // 2
+    piece = half // PIECES
+    modes = t_lon.shape[1]
+    wide = chans * own
+    hid = up.shape[-1]
+
+    def lat_peer(k):
+        return lax.rem(lat + k, lats)
+
+    def ch_peer(k):
+        return lax.rem((partner if k % 2 else ch) + k - k % 2, chans)
+
+    def ch_source(k):
+        return lax.rem((partner if k % 2 else ch) + chans - (k - k % 2), chans)
+
+    def half_of(k):
+        return 1 - core if k % 2 else core
+
+    far_first = tuple(range(2, chans)) + (1,)
+
+    barrier = pltpu.get_barrier_semaphore()
+    for k in range(1, lats):
+        pl.semaphore_signal(barrier, inc=1, device_id={"lat": lat_peer(k)}, device_id_type=MESH)
+    for k in range(1, chans):
+        pl.semaphore_signal(barrier, inc=1, device_id={"ch": ch_peer(k)}, device_id_type=MESH)
+
+    def copy(kind, k, source, target, device):
+        return pltpu.make_async_remote_copy(
+            src_ref=source,
+            dst_ref=target,
+            send_sem=send_sem.at[kind, k],
+            recv_sem=recv_sem.at[kind, k],
+            device_id=device,
+            device_id_type=MESH,
+        )
+
+    gain = gains[...].astype(F32)
+    shift = shifts[...].astype(F32)
+    bias_send[...] = jnp.broadcast_to(up_bias[...].astype(F32), bias_send.shape)
+    x[...] = jnp.zeros_like(x)
+    for r in range(rows):
+        x[r * padded : r * padded + width] = state[r]
+    for layer, weights in enumerate((fin, fout)):
+        for i in range(2):
+            mixing[layer, i, 0], mixing[layer, i, 1] = halves(weights[i])
+    pl.semaphore_wait(barrier, lats + chans - 2)
+    setup = [
+        copy(2, 0, bias_send, bias_recv, {"ch": partner}),
+        copy(3, 0, up, up_recv, {"ch": partner}),
+        copy(4, 0, down, down_recv, {"ch": partner}),
+    ]
+    lane = lax.broadcasted_iota(jnp.int32, (x.shape[0], 128), 1)
+
+    def start(copies):
+        for each in copies:
+            each.start()
+        return copies
+
+    def finish(copies):
+        for each in copies:
+            each.wait()
+
+    def norm_terms(kind, extra):
+        values = x[...]
+        total = jnp.sum(values, -1, keepdims=True)
+        squares = jnp.sum(values * values, -1, keepdims=True)
+        packed = jnp.where(lane == 0, total, jnp.where(lane == 1, squares, 0.0))
+        stat_send[kind] = jnp.transpose(packed)[0:8]
+        copies = start(
+            [
+                copy(kind, lats + k, stat_send.at[kind], stat_recv.at[kind, k], {"ch": ch_peer(k)})
+                for k in range(1, chans)
+            ]
+        )
+        start(extra)
+        finish(copies)
+        total = stat_send[kind]
+        for k in range(1, chans):
+            total = total + stat_recv[kind, k]
+        total = jnp.transpose(total)
+        mean = total[:, 0:1] / wide
+        return mean, lax.rsqrt(total[:, 1:2] / wide - mean * mean + EPS)
+
+    def step(first):
+        mean, scaled = norm_terms(0, setup if first else [])
+        for r in range(rows):
+            part = slice(r * padded, (r + 1) * padded)
+            now = x[part]
+            normed = (now - mean[part]) * scaled[part] * gain[0:1] + shift[0:1]
+            x[part] = now + normed
+            high, low = halves(normed)
+            spectra = dot(t_lon[0], high) + dot(t_lon[0], low) + dot(t_lon[1], high)
+            lon_send[:, r] = spectra.astype(BF16).reshape(lats, modes // lats, own)
+        copies = start(
+            [
+                copy(0, k, lon_send.at[lat_peer(k)], lon_recv.at[lat], {"lat": lat_peer(k)})
+                for k in range(1, lats)
+            ]
+        )
+        lon_recv[pl.ds(lat, 1)] = lon_send[pl.ds(lat, 1)]
+        finish(copies)
+        data = lon_recv[...].reshape(-1, own)
+        spec = dot(t_lat[0], data) + dot(t_lat[1], data)
+        split = spec.shape[0] // 2
+
+        def complex_apply(pair, layer, bias):
+            high, low = halves(pair)
+            one, two = (
+                dot(high, mixing[layer, i, 0])
+                + dot(low, mixing[layer, i, 0])
+                + dot(high, mixing[layer, i, 1])
+                for i in range(2)
+            )
+            return (one[:split] - two[split:] + bias[0:1], one[split:] + two[:split] + bias[1:2])
+
+        real, imag = complex_apply(spec, 0, fin_bias)
+        pair = jnp.concatenate((jnp.maximum(real, 0.0), jnp.maximum(imag, 0.0)), 0)
+        real, imag = complex_apply(pair, 1, fout_bias)
+        high, low = halves(jnp.concatenate((soft_shrink(real), soft_shrink(imag)), 0))
+        back = dot(t_rows[0], high) + dot(t_rows[0], low) + dot(t_rows[1], high)
+        row_send[...] = back.astype(BF16).reshape(row_send.shape)
+        copies = start(
+            [
+                copy(1, k, row_send.at[lat_peer(k)], row_recv.at[lat], {"lat": lat_peer(k)})
+                for k in range(1, lats)
+            ]
+        )
+        row_recv[pl.ds(lat, 1)] = row_send[pl.ds(lat, 1)]
+        finish(copies)
+        for r in range(rows):
+            part = slice(r * padded, (r + 1) * padded)
+            data = row_recv[:, r].reshape(-1, own)
+            x[part] = x[part] + dot(t_back[0], data) + dot(t_back[1], data)
+        mean, scaled = norm_terms(1, [])
+        for p in range(PIECES):
+            for h in range(2):
+                part = slice(h * half + p * piece, h * half + (p + 1) * piece)
+                normed = (x[part] - mean[part]) * scaled[part] * gain[1:2] + shift[1:2]
+                tok_send[h, p] = normed.astype(BF16)
+        tokens = [
+            {
+                k: copy(
+                    5 + p, k, tok_send.at[half_of(k), p], tok_recv.at[p, k], {"ch": ch_peer(k)}
+                )
+                for k in far_first
+            }
+            for p in range(PIECES)
+        ]
+        for p in range(PIECES):
+            start(tokens[p].values())
+        if first:
+            finish(setup)
+        results = []
+        chunk = 256
+        blocks = [(s, lo) for s in range(2) for lo in range(0, hid, chunk)]
+        for p in range(PIECES):
+            tok_recv[p, 0] = tok_send[core, p]
+            tokens[p][1].wait_recv()
+            for s, lo in blocks:
+                weight, bias = ((up, bias_send), (up_recv, bias_recv))[s]
+                cut = slice(lo, lo + chunk)
+                pre = bias[0:1, cut]
+                for k in range(2):
+                    pre = pre + dot(tok_recv[p, k], weight[ch_source(k), :, cut])
+                partial[s, :, cut] = pre
+            for k in range(2, chans):
+                tokens[p][k].wait_recv()
+            for s, lo in blocks:
+                weight = (up, up_recv)[s]
+                cut = slice(lo, lo + chunk)
+                pre = partial[s, :, cut]
+                for k in range(2, chans):
+                    pre = pre + dot(tok_recv[p, k], weight[ch_source(k), :, cut])
+                hidden[s, :, cut] = gelu(pre).astype(BF16)
+            for k in far_first + (0,):
+                peer = ch_peer(k)
+                mixed = dot(hidden[0], down[peer]) + dot(hidden[1], down_recv[peer])
+                if k:
+                    mix_send[p, k] = mixed.astype(BF16)
+                    each = copy(
+                        5 + PIECES + p, k, mix_send.at[p, k], mix_recv.at[p, k], {"ch": peer}
+                    )
+                    each.start()
+                    results.append(each)
+                else:
+                    mix_recv[p, 0] = mixed.astype(BF16)
+        for p in range(PIECES):
+            for each in tokens[p].values():
+                each.wait_send()
+        finish(results)
+        for p in range(PIECES):
+            for h in range(2):
+                begin = pl.multiple_of(half_of(h) * half + p * piece, 16)
+                mixed = shift[2:3]
+                for k in range(h, chans, 2):
+                    mixed = mixed + mix_recv[p, k].astype(F32)
+                x[pl.ds(begin, piece)] = x[pl.ds(begin, piece)] + mixed
+
+    step(True)
+
+    @pl.loop(1, STEPS)
+    def _(_index):
+        step(False)
+
+    for r in range(rows):
+        out[r] = x[r * padded : r * padded + width]
+
+
+def block_diagonal(weights):
+    parts, blocks, size, _ = weights.shape
+    eye = jnp.eye(blocks, dtype=weights.dtype)
+    spread = weights[:, :, :, None, :] * eye[None, :, None, :, None]
+    return spread.reshape(parts, blocks * size, blocks * size)
+
+
+def fused(
+    lats,
+    chans,
+    state,
+    norm_gains,
+    channel_biases,
+    filter_in,
+    filter_in_bias,
+    filter_out,
+    filter_out_bias,
+    up_weight,
+    up_bias,
+    down_weight,
+):
+    _, rows, width, own = state.shape
+    padded = -(-width // 32) * 32
+    share = 2 * M // lats
+    piece = rows * padded // 2 // PIECES
+    hid = up_weight.shape[1]
+    tables = fourier_tables(width, padded, rows * lats, M, lats)
+    down = down_weight.reshape(hid, chans, own).transpose(1, 0, 2)
+    args = (
+        state[0],
+        norm_gains,
+        channel_biases,
+        block_diagonal(filter_in),
+        filter_in_bias.reshape(2, own),
+        block_diagonal(filter_out),
+        filter_out_bias.reshape(2, own),
+        up_weight.reshape(chans, own, hid),
+        up_bias.reshape(1, hid),
+        down,
+    ) + tuple(jnp.asarray(t) for t in tables)
+    vmem = pl.BlockSpec(memory_space=pltpu.VMEM)
+    spectrum = (lats, rows, share, own)
+    result = pl.pallas_call(
+        functools.partial(rollout, lats, chans),
+        out_shape=jax.ShapeDtypeStruct((rows, width, own), F32),
+        in_specs=[vmem] * len(args),
+        out_specs=vmem,
+        scratch_shapes=[
+            pltpu.VMEM((rows * padded, own), F32),
+            pltpu.VMEM((2, 8, rows * padded), F32),
+            pltpu.VMEM((2, chans, 8, rows * padded), F32),
+            pltpu.VMEM(spectrum, BF16),
+            pltpu.VMEM(spectrum, BF16),
+            pltpu.VMEM(spectrum, BF16),
+            pltpu.VMEM(spectrum, BF16),
+            pltpu.VMEM((2, PIECES, piece, own), BF16),
+            pltpu.VMEM((PIECES, chans, piece, own), BF16),
+            pltpu.VMEM((PIECES, chans, piece, own), BF16),
+            pltpu.VMEM((PIECES, chans, piece, own), BF16),
+            pltpu.VMEM((8, hid), F32),
+            pltpu.VMEM((8, hid), F32),
+            pltpu.VMEM((chans, own, hid), BF16),
+            pltpu.VMEM(down.shape, BF16),
+            pltpu.VMEM((2, piece, hid), F32),
+            pltpu.VMEM((2, piece, hid), BF16),
+            pltpu.VMEM((2, 2, 2, own, own), BF16),
+            pltpu.SemaphoreType.DMA((5 + 2 * PIECES, lats + chans)),
+            pltpu.SemaphoreType.DMA((5 + 2 * PIECES, lats + chans)),
+        ],
+        compiler_params=pltpu.CompilerParams(
+            collective_id=0, has_side_effects=True, vmem_limit_bytes=48 * 1024 * 1024
+        ),
+    )(*args)
+    return result[None]
+
+
+def dispatch(sizes, *args):
+    lats, chans = sizes["lat"], sizes["ch"]
+    aligned = args[0].shape[1] * (-(-args[0].shape[2] // 32)) * 32 % (32 * PIECES) == 0
+    if 2 * M // lats % 16 == 0 and chans % 2 == 0 and aligned:
+        return fused(lats, chans, *args)
+    return local(*args)
+
+
 def solution(mesh):
     placed = (
         P(None, "lat", None, "ch"),
@@ -171,5 +558,5 @@
         P("ch", None),
     )
     return jax.shard_map(
-        local, mesh=mesh, in_specs=placed, out_specs=P(None, "lat", None, "ch"), check_vma=False
-    )
+        functools.partial(dispatch, dict(mesh.shape)), mesh=mesh, in_specs=placed, out_specs=P(None, "lat", None, "ch"), check_vma=False
+    )

time: 457 us -> 168 us (0.37); the launches traced: 448 us -> 168 us
  blocking collectives: 222 us -> 0 us
  Pallas kernels: 0 us -> 156 us
  matrix products: 72.4 us -> 0 us
  local copies, waits for them, and re-layouts: 69.2 us -> 11.8 us
  other arithmetic: 36.9 us -> 0.07 us
  waiting for transfers between devices: 19.4 us -> 0 us
  between operations: 15.4 us -> 0.16 us
  starting transfers between devices: 13 us -> 0 us
    all_to_all x13 -> x0, blocking collectives: 169 us -> none  [the longest x3 47.8 us: local(): lax.all_to_all(jnp.stack((real_lon, imag_lon)), 'lat', split_axis=3, conc...]
    pallas_call x0 -> x1, Pallas kernels: none -> 156 us  [fused(): pl.pallas_call(functools.partial(rollout, lats, chans), out_shape=jax.Sha...]
    dot_general x84 -> x0, matrix products: 72.4 us -> none  [the longest x4 34.7 us: local(): jnp.dot(hidden, full_down, preferred_element_type=jnp.float32)]
    all_to_all x32 -> x0, local copies, waits for them, and re-layouts: 28.2 us -> none  [the longest x12 24.4 us: local(): lax.all_to_all(mixed.reshape(owned.shape), 'ch', split_axis=3, concat_axi...]
    all_gather x3 -> x0, blocking collectives: 27 us -> none  [the longest x1 16.5 us: local(): lax.all_gather(up_bias, 'ch', axis=0, tiled=True)]
    psum x4 -> x0, blocking collectives: 26.2 us -> none  [local(): lax.psum((jnp.sum(values, -1, keepdims=True), jnp.sum(values * values, -1...]
    unnamed x4 -> x0, other arithmetic: 20.4 us -> none
    all_to_all x3 -> x0, starting transfers between devices: 13 us -> none  [the longest x1 5.84 us: local(): lax.all_to_all(jnp.stack((real_lon, imag_lon)), 'lat', split_axis=3, conc...]
  transfers between devices with their start and end apart: 5 -> 0, of which waited for: 3 -> 0; matrix products, arithmetic and copies ran while one was open for 4% -> 0% of each run, Pallas kernels for 0% -> 0%
where the time goes in v1:
time: 168 us
  Pallas kernels  156 us (93%)
  local copies, waits for them, and re-layouts  11.8 us (7%)
    pallas_call x1, Pallas kernels, fused(): pl.pallas_call(functools.partial(rollout, lats, chans), out_shape=jax.Sha...  156 us
    unnamed x22, local copies, waits for them, and re-layouts  6.89 us

profile of v1, /device:TPU:0, one launch (start us, length us, event | category | flops | bytes accessed | tf_op | source)
XLA Modules:
  0.0 168.0 jit_solution(6864584185466664835)
XLA Ops:
  0.0 0.0 copy-start.7
  0.0 1.1 mul.40
  1.1 0.2 mul.41
  1.4 0.0 copy-done.7
  1.4 0.1 mul.46
  1.5 0.2 mul.47
  1.8 0.1 mul.42
  1.9 0.2 mul.43
  2.0 0.1 broadcast_multiply_fusion
  2.1 1.6 copy.16
  3.7 0.0 copy-start.8
  3.7 0.0 copy-start.9
  3.7 0.0 copy-start.5
  3.7 0.0 copy-start.6
  3.7 0.7 copy.17
  4.4 0.0 copy-start.1
  4.4 1.2 copy.21
  5.6 0.0 copy-done.8
  5.6 0.0 copy-done.9
  5.6 0.1 reshape.31.fin_bias
  5.7 0.8 reshape.32.fout_bias
  6.5 0.0 copy-done.5
  6.5 0.0 copy-done.6
  6.5 0.0 copy-done.1
  6.5 0.0 copy-start
  6.5 1.3 copy-done
  7.8 0.0 copy-start.2
  7.8 1.1 copy-done.2
  8.8 0.9 copy-done.3
  9.7 0.9 copy-done.4
  10.6 156.0 %shard_map.136 = f32[3,180,192]{2,1,0:T(8,128)S(1)} custom-call(f32[3,180,192]{2,1,0:T(8,128)S(1)} %bitcast.9, bf16[2,192]{1,0:T(2,128)(2,1)S(1)} %copy-done.6, bf16[3,192]{1,0:T(4,128)(2,1)S(1)} %copy-done.5, f32[2,192,192]{2,1,0:T(8,128)S(1)} %get-tuple-element.6.fin, f32[2,192]{1,0:T(2,128)S(1)} %reshape.31.fin_bias, ...), custom_call_target="tpu_custom_call" | custom-call | tf_op jit(solution)/shard_map/pallas_call | solution.py:505
  166.6 1.4 copy.18
  (4 shorter events, 0.0 us)
Async XLA Ops:
  0.0 1.4 copy-start.7
  3.7 1.9 %copy-start.8 = (bf16[768]{0:T(1024)(128)(2,1)S(1)}, bf16[768]{0:T(1024)(128)(2,1)}, u32[]{:S(2)}) copy-start(bf16[768]{0:T(1024)(128)(2,1)} %param.22) | copy-start | bytes 4612
  3.7 1.9 %copy-start.9 = (f32[2,2,96]{2,1,0:T(2,128)S(1)}, f32[2,2,96]{2,1,0:T(2,128)}, u32[]{:S(2)}) copy-start(f32[2,2,96]{2,1,0:T(2,128)} %param.18) | copy-start | bytes 4612
  3.7 2.8 %copy-start.5 = (bf16[3,192]{1,0:T(4,128)(2,1)S(1)}, bf16[3,192]{1,0:T(4,128)(2,1)}, u32[]{:S(2)}) copy-start(bf16[3,192]{1,0:T(4,128)(2,1)} %shifts.1) | copy-start | bytes 3460
  3.7 2.8 %copy-start.6 = (bf16[2,192]{1,0:T(2,128)(2,1)S(1)}, bf16[2,192]{1,0:T(2,128)(2,1)}, u32[]{:S(2)}) copy-start(bf16[2,192]{1,0:T(2,128)(2,1)} %gains.1) | copy-start | bytes 2308
  4.4 2.1 %copy-start.1 = (bf16[2,384,384]{2,1,0:T(8,128)(2,1)S(1)}, bf16[2,384,384]{2,1,0:T(8,128)(2,1)}, u32[]{:S(2)}) copy-start(bf16[2,384,384]{2,1,0:T(8,128)(2,1)} %constant.10.clone.t_rows) | copy-start | bytes 1769476
  6.5 1.3 copy-start
  7.8 1.1 copy-start.2
  8.8 0.9 copy-start.3
  9.7 0.9 copy-start.4

commit v2 on v1

--- a/solution.py
+++ b/solution.py
@@ -161,7 +161,7 @@
     return values
 
 
-PIECES = 2
+PIECES = 3
 F32 = jnp.float32
 BF16 = jnp.bfloat16
 MESH = pl.DeviceIdType.MESH

time: 168 us -> 167 us (level)
  no operation moved by 1% of the time
where the time goes in v2:
time: 167 us
  Pallas kernels  155 us (93%)
  local copies, waits for them, and re-layouts  11.8 us (7%)
    pallas_call x1, Pallas kernels, fused(): pl.pallas_call(functools.partial(rollout, lats, chans), out_shape=jax.Sha...  155 us
    unnamed x22, local copies, waits for them, and re-layouts  6.89 us

profile of v2, /device:TPU:0, one launch (start us, length us, event | category | flops | bytes accessed | tf_op | source)
XLA Modules:
  0.0 167.1 jit_solution(10117641787235602315)
XLA Ops:
  0.0 0.0 copy-start.7
  0.0 1.1 mul.40
  1.1 0.2 mul.41
  1.4 0.0 copy-done.7
  1.4 0.1 mul.46
  1.5 0.2 mul.47
  1.8 0.1 mul.42
  1.9 0.2 mul.43
  2.0 0.1 broadcast_multiply_fusion
  2.1 1.6 copy.16
  3.7 0.0 copy-start.8
  3.7 0.0 copy-start.9
  3.7 0.0 copy-start.5
  3.7 0.0 copy-start.6
  3.7 0.7 copy.17
  4.4 0.0 copy-start.1
  4.4 1.2 copy.21
  5.6 0.0 copy-done.8
  5.6 0.0 copy-done.9
  5.6 0.1 reshape.31.fin_bias
  5.7 0.8 reshape.32.fout_bias
  6.5 0.0 copy-done.5
  6.5 0.0 copy-done.6
  6.5 0.0 copy-done.1
  6.5 0.0 copy-start
  6.5 1.3 copy-done
  7.8 0.0 copy-start.2
  7.8 1.1 copy-done.2
  8.8 0.9 copy-done.3
  9.7 0.9 copy-done.4
  10.6 155.1 %shard_map.136 = f32[3,180,192]{2,1,0:T(8,128)S(1)} custom-call(f32[3,180,192]{2,1,0:T(8,128)S(1)} %bitcast.9, bf16[2,192]{1,0:T(2,128)(2,1)S(1)} %copy-done.6, bf16[3,192]{1,0:T(4,128)(2,1)S(1)} %copy-done.5, f32[2,192,192]{2,1,0:T(8,128)S(1)} %get-tuple-element.6.fin, f32[2,192]{1,0:T(2,128)S(1)} %reshape.31.fin_bias, ...), custom_call_target="tpu_custom_call" | custom-call | tf_op jit(solution)/shard_map/pallas_call | solution.py:505
  165.7 1.4 copy.18
  (4 shorter events, 0.0 us)
Async XLA Ops:
  0.0 1.4 copy-start.7
  3.7 1.9 %copy-start.8 = (bf16[768]{0:T(1024)(128)(2,1)S(1)}, bf16[768]{0:T(1024)(128)(2,1)}, u32[]{:S(2)}) copy-start(bf16[768]{0:T(1024)(128)(2,1)} %param.22) | copy-start | bytes 4612
  3.7 1.9 %copy-start.9 = (f32[2,2,96]{2,1,0:T(2,128)S(1)}, f32[2,2,96]{2,1,0:T(2,128)}, u32[]{:S(2)}) copy-start(f32[2,2,96]{2,1,0:T(2,128)} %param.18) | copy-start | bytes 4612
  3.7 2.8 %copy-start.5 = (bf16[3,192]{1,0:T(4,128)(2,1)S(1)}, bf16[3,192]{1,0:T(4,128)(2,1)}, u32[]{:S(2)}) copy-start(bf16[3,192]{1,0:T(4,128)(2,1)} %shifts.1) | copy-start | bytes 3460
  3.7 2.8 %copy-start.6 = (bf16[2,192]{1,0:T(2,128)(2,1)S(1)}, bf16[2,192]{1,0:T(2,128)(2,1)}, u32[]{:S(2)}) copy-start(bf16[2,192]{1,0:T(2,128)(2,1)} %gains.1) | copy-start | bytes 2308
  4.4 2.1 %copy-start.1 = (bf16[2,384,384]{2,1,0:T(8,128)(2,1)S(1)}, bf16[2,384,384]{2,1,0:T(8,128)(2,1)}, u32[]{:S(2)}) copy-start(bf16[2,384,384]{2,1,0:T(8,128)(2,1)} %constant.10.clone.t_rows) | copy-start | bytes 1769476
  6.5 1.3 copy-start
  7.8 1.1 copy-start.2
  8.8 0.9 copy-start.3
  9.7 0.9 copy-start.4
